TPU v7x, 256 devices: a whole 4x4x8 slice. The times are simulated.
256 devices in a mesh: row: 16 (over x, y), col: 16 (over z, core).
Axes of the slice: x: 4, y: 4, z: 8, core: 2. Of those that a mesh axis runs over, the one named last changes fastest.
Arguments:
- points: bfloat16 [40960, 64], P(('row', 'col')), may hold values from -5 to 5
- start_vectors: bfloat16 [40960, 32], P(('row', 'col')), may hold values from -12 to 12
Outputs:
- basis: float32 [40960, 32], P(('row', 'col'))
All inputs are finite; a program needn't handle non-finite values.
Results may differ from a plain program's by a relative error of at most 0.007.
Values may be sent and summed in bfloat16 or wider, within the bound.
No kernel may reach another device: no remote copies, remote signals or barrier semaphores. Data moves between devices by JAX's collectives and lax.ppermute only.
A program may use at most 64 MiB of HBM per device.

v0:
```python
import math

import jax
import jax.numpy as jnp
from jax import lax
from jax.experimental import pallas as pl
from jax.experimental.pallas import tpu as pltpu
from jax.sharding import Mesh
from jax.sharding import PartitionSpec as P

KERNEL_SCALE = 5.12
F32 = jnp.float32
BF16 = jnp.bfloat16
LANES = 128
PARAMS = pltpu.CompilerParams(vmem_limit_bytes=32 * 1024 * 1024)
REST = 32
WIDTH = 512
NORM, ONES, END = 64, 67, 70


def lane_of(shape):
    return lax.broadcasted_iota(jnp.int32, shape, len(shape) - 1)


def row_of(shape):
    return lax.broadcasted_iota(jnp.int32, shape, len(shape) - 2)


def roll(x, shift):
    shift %= LANES
    return pltpu.roll(x, shift, 1) if shift else x


def fold(x, place=0):
    h = x.shape[0] // 4
    group = lane_of((h, LANES)) // REST
    out = jnp.zeros((h, LANES), F32)
    for g in range(4):
        out = jnp.where(group == g, roll(x[g * h : (g + 1) * h], REST * (g - place)), out)
    return out


def unfold(pieces):
    h = pieces[0].shape[0]
    group = lane_of((h, LANES)) // REST
    rows = []
    for g in range(4):
        out = jnp.zeros((h, LANES), F32)
        for q, piece in enumerate(pieces):
            out = jnp.where(group == q, roll(piece, REST * (q - g)), out)
        rows.append(out)
    return jnp.concatenate(rows, axis=0)


def split(x):
    first = x.astype(BF16).astype(F32)
    second = (x - first).astype(BF16).astype(F32)
    return first, second, x - first - second


def widen(x):
    return jnp.concatenate([x, jnp.zeros((x.shape[0], LANES - x.shape[1]), x.dtype)], axis=1)


def main_and_rest(x):
    return x[:, 0:LANES], fold(widen(x[:, LANES : LANES + REST]))


def copies(ref, value):
    for i in range(ref.shape[0]):
        ref[i] = value


def pack_body(points_hbm, vectors_hbm, cols_hbm, rows_ref, points_ref, vectors_ref, block_ref, sems):
    loads = (
        pltpu.make_async_copy(points_hbm, points_ref, sems.at[0]),
        pltpu.make_async_copy(vectors_hbm, vectors_ref, sems.at[1]),
    )
    for load in loads:
        load.start()
    loads[0].wait()
    pts = points_ref[...].astype(F32)
    group = pts.shape[1]
    main, rest = main_and_rest(pts)
    rows_ref[...] = jnp.concatenate([main, rest], axis=0).astype(BF16)
    flat = jnp.concatenate([main, widen(pts[:, LANES:])], axis=1)
    norm = jnp.sum(flat * flat, axis=0, keepdims=True) * -0.5
    row = row_of((8, flat.shape[1]))
    extra = jnp.where((row >= ONES - NORM) & (row < END - NORM), 1.0, 0.0)
    for k, piece in enumerate(split(norm)):
        extra = jnp.where(row == k, piece, extra)
    blank = jnp.zeros((LANES - NORM - 8, flat.shape[1]), F32)
    flat = jnp.concatenate([flat, extra, blank], axis=0).T[0:group]
    loads[1].wait()
    main, rest = main_and_rest(vectors_ref[...].astype(F32))
    block_ref[...] = jnp.concatenate([flat, main, rest], axis=0).astype(BF16)
    count = cols_hbm.shape[0]
    sends = [
        pltpu.make_async_copy(block_ref, cols_hbm.at[i], sems.at[2 + i]) for i in range(count)
    ]
    for send in sends:
        send.start()
    for send in sends:
        send.wait()


def blocks_of(count):
    lanes = count * LANES
    main = [(at, WIDTH) for at in range(0, lanes, WIDTH)]
    return main, (lanes, lanes // 4)


def put_columns(cols_ref, left_ref, vec_ref):
    count = cols_ref.shape[0]
    total = left_ref.shape[0]
    for i in range(count):
        left_ref[i * LANES : (i + 1) * LANES, :] = cols_ref[i, 0:128]
        at = count * LANES + i * REST
        left_ref[at : at + REST, :] = cols_ref[i, 128:160]
    vec_ref[32:48, :] = jnp.where(row_of((16, total)) == 0, 1.0, 0.0).astype(BF16)
    for i in range(count):
        vec_ref[0:32, i * LANES : (i + 1) * LANES] = cols_ref[i, 160:192]
    for m in range(count // 4):
        rests = [cols_ref[4 * m + q, 192:200].astype(F32) for q in range(4)]
        at = (count + m) * LANES
        vec_ref[0:32, at : at + LANES] = unfold(rests).astype(BF16)


def put_rows(rows_ref, core, right_ref):
    count = rows_ref.shape[0] // 2

    def put(tile, raw):
        at = tile * LANES
        norm = jnp.sum(raw * raw, axis=0, keepdims=True) * -0.5
        row = row_of((16, LANES))
        extra = jnp.where(row < ONES - NORM, 1.0, 0.0)
        for i, piece in enumerate(split(norm)):
            extra = jnp.where(row == ONES - NORM + i, piece, extra)
        right_ref[0:64, at : at + LANES] = raw.astype(BF16)
        right_ref[64:80, at : at + LANES] = extra.astype(BF16)
        right_ref[80:128, at : at + LANES] = jnp.zeros((48, LANES), BF16)

    for i in range(count):
        put(i, rows_ref[2 * i + core, 0:64].astype(F32))
    for m in range(count // 4):
        rests = [rows_ref[2 * (4 * m + q) + core, 64:80].astype(F32) for q in range(4)]
        put(count + m, unfold(rests))


def affinity_product(log_scale, left_ref, right_ref, vec_ref, aff_ref, send_ref):
    total = left_ref.shape[0]
    main, rest = blocks_of(send_ref.shape[0])
    chunk = 640

    def weights(at, width):
        right = right_ref[:, at : at + width]
        for start in range(0, total, chunk):
            left = left_ref[start : start + chunk, :]
            power = jnp.dot(left, right, preferred_element_type=F32) * log_scale
            aff_ref[start : start + chunk, at : at + width] = jnp.exp2(power).astype(BF16)

    def product(at, width):
        return jnp.dot(
            vec_ref[...], aff_ref[:, at : at + width], preferred_element_type=F32
        )

    def send_main(at, width):
        out = product(at, width)
        for k in range(width // LANES):
            tile = out[:, k * LANES : (k + 1) * LANES]
            send_ref[at // LANES + k, 0:32, :] = tile[0:32]
            send_ref[at // LANES + k, 40:41, :] = tile[32:33]

    def send_rest(at, width):
        out = product(at, width)
        row = row_of((8, LANES))
        for m in range(width // LANES):
            tile = out[:, m * LANES : (m + 1) * LANES]
            for q in range(4):
                send_ref[4 * m + q, 32:40, :] = fold(tile[0:32], q)
                degree = jnp.broadcast_to(roll(tile[32:40], -REST * q)[0:1], (8, LANES))
                send_ref[4 * m + q, 40:48, :] = jnp.where(row == 1, degree, 0.0)

    weights(*main[0])
    weights(*rest)
    send_rest(*rest)
    send_main(*main[0])
    for block in main[1:]:
        weights(*block)
        send_main(*block)


def away_body(log_scale):
    def body(right_ref, cols_ref, aff_ref, send_ref, left_ref, vec_ref):
        put_columns(cols_ref, left_ref, vec_ref)
        affinity_product(log_scale, left_ref, right_ref, vec_ref, aff_ref, send_ref)

    return body


def home_body(log_scale):
    def body(left_ref, right_ref, vec_ref, aff_ref, send_ref):
        affinity_product(log_scale, left_ref, right_ref, vec_ref, aff_ref, send_ref)

    return body


def rows_body(rows_ref, away_right_ref, home_right_ref):
    core = lax.axis_index("core")
    put_rows(rows_ref, 1 - core, away_right_ref)
    put_rows(rows_ref, core, home_right_ref)


def join_body(mine_ref, other_ref, out_ref):
    out_ref[...] = mine_ref[...] + other_ref[...]


def gram_of(x):
    return lax.dot_general(
        x,
        x,
        (((1,), (1,)), ((), ())),
        precision=lax.Precision.HIGHEST,
        preferred_element_type=F32,
    )


def whole(main, rest):
    return jnp.concatenate([main, unfold([rest])], axis=1)


def scale_body(recv_ref, spread_ref, degree_ref):
    total = jnp.sum(recv_ref[...], axis=0)
    rest = jnp.where(lane_of((1, LANES)) < REST, total[41:42], 0.0)
    rest = jnp.broadcast_to(rest, (8, LANES))
    rest = (rest + roll(rest, REST)) + (roll(rest, 2 * REST) + roll(rest, 3 * REST))
    degree_ref[0:8, :] = jnp.broadcast_to(total[40:41], (8, LANES))
    degree_ref[8:16, :] = rest
    main, rest = total[0:32] / total[40:41], total[32:40] / rest
    copies(spread_ref, jnp.concatenate([main, rest], axis=0))


def put_vectors(spread_ref, vec_ref):
    count = spread_ref.shape[0]

    def put(tile, value):
        first = value.astype(BF16)
        at = tile * LANES
        vec_ref[0:32, at : at + LANES] = first
        vec_ref[32:64, at : at + LANES] = (value - first.astype(F32)).astype(BF16)

    for i in range(count):
        put(i, spread_ref[i, 0:32, :])
    for m in range(count // 4):
        put(count + m, unfold([spread_ref[4 * m + q, 32:40, :] for q in range(4)]))


def second_product(aff_ref, vec_ref, send_ref):
    main, rest = blocks_of(send_ref.shape[0])

    def product(at, width):
        out = jnp.dot(vec_ref[...], aff_ref[:, at : at + width], preferred_element_type=F32)
        return out[0:32] + out[32:64]

    out = product(*rest)
    for m in range(rest[1] // LANES):
        for q in range(4):
            send_ref[4 * m + q, 32:40, :] = fold(out[:, m * LANES : (m + 1) * LANES], q)
    for at, width in main:
        out = product(at, width)
        for k in range(width // LANES):
            send_ref[at // LANES + k, 0:32, :] = out[:, k * LANES : (k + 1) * LANES]


def put_gram(gram, send_ref):
    for i in range(send_ref.shape[0]):
        send_ref[i, 40:48, :] = gram


def away_again_body(aff_ref, spread_ref, send_ref, vec_ref, gram_ref):
    put_vectors(spread_ref, vec_ref)
    vec = vec_ref[...]
    gram = lax.dot_general(vec, vec, (((1,), (1,)), ((), ())), preferred_element_type=F32)
    gram = gram[0:32] + gram[32:64]
    gram = fold(widen(gram[:, 0:32] + gram[:, 32:64]))
    gram_ref[...] = gram
    second_product(aff_ref, vec_ref, send_ref)
    put_gram(gram, send_ref)


def home_again_body(aff_ref, vec_ref, gram_ref, send_ref):
    second_product(aff_ref, vec_ref, send_ref)
    put_gram(gram_ref[...], send_ref)


def solved(gram, right):
    size = 4 * gram.shape[0]
    wide = right.shape[1] // LANES
    columns = [
        jnp.concatenate(
            [
                jnp.broadcast_to(gram[:, REST * g + k : REST * g + k + 1], (8, LANES))
                for g in range(k // 8, 4)
            ],
            axis=0,
        )
        for k in range(size)
    ]
    rows = [right[8 * g : 8 * g + 8] for g in range(size // 8)]
    for j in range(size):
        base, at = j // 8, j % 8
        pivot = columns[j][at : at + 1]
        scale = lax.rsqrt(pivot)
        scale = scale * (1.5 - 0.5 * pivot * scale * scale)
        factor = columns[j] * scale
        for k in range(j + 1, size):
            skip = 8 * (k // 8 - base)
            mine = factor[k - 8 * base : k - 8 * base + 1]
            columns[k] = columns[k] - factor[skip:] * mine
        top = rows[base][at : at + 1] * jnp.concatenate([scale] * wide, axis=1)
        for g in range(base, size // 8):
            part = factor[8 * (g - base) : 8 * (g - base) + 8]
            if g == base:
                row = row_of((8, LANES))
                part = jnp.where(row > at, part, 0.0)
            new = rows[g] - jnp.concatenate([part] * wide, axis=1) * top
            if g == base:
                new = jnp.where(row_of(new.shape) == at, top, new)
            rows[g] = new
    return jnp.concatenate(rows, axis=0)


def middle_body(points):
    def body(recv_ref, degree_ref, scaled_ref, gram_ref):
        total = jnp.sum(recv_ref[...], axis=0)
        main = total[0:32] / degree_ref[0:1, :]
        rest = total[32:40] / degree_ref[8:16, :]
        scaled = solved(total[40:48] / points, whole(main, rest))
        scaled_ref[...] = scaled
        copies(gram_ref, fold(widen(gram_of(scaled))))

    return body


def again_body(recv_ref, gram_ref):
    copies(gram_ref, jnp.sum(recv_ref[...], axis=0))


def last_body(points):
    def body(recv_ref, scaled_ref, out_ref):
        gram = jnp.sum(recv_ref[...], axis=0) / points
        out_ref[...] = solved(gram, scaled_ref[...])[:, 0 : out_ref.shape[1]]

    return body


def shards(points, start_vectors):
    group, features = points.shape
    row, half, cores = lax.axis_size("row"), lax.axis_size("z"), lax.axis_size("core")
    col = half * cores
    total = group * row * col
    log_scale = 2.0 * KERNEL_SCALE / features * math.log2(math.e)
    lanes = half * group
    right_shape = pltpu.VMEM((LANES, lanes), BF16)
    shape = jax.ShapeDtypeStruct

    def exchange(x, axis):
        return lax.all_to_all(x, axis, 0, 0, tiled=True)

    def swap(x):
        return lax.ppermute(x, "core", [(0, 1), (1, 0)])

    def call(body, out_shape, *args, scratch=(), **kwargs):
        return pl.pallas_call(
            body, out_shape=out_shape, scratch_shapes=scratch, compiler_params=PARAMS, **kwargs
        )(*args)

    hbm_space = pl.BlockSpec(memory_space=pltpu.HBM)
    cols, rows = call(
        pack_body,
        (shape((row, group + 40, LANES), BF16), pltpu.VMEM((80, LANES), BF16)),
        pltpu.with_memory_space_constraint(points.T, pltpu.HBM),
        pltpu.with_memory_space_constraint(start_vectors.T, pltpu.HBM),
        scratch=(
            pltpu.VMEM((features, group), BF16),
            pltpu.VMEM((start_vectors.shape[1], group), BF16),
            pltpu.VMEM((group + 40, LANES), BF16),
            pltpu.SemaphoreType.DMA((2 + row,)),
        ),
        in_specs=[hbm_space, hbm_space],
        out_specs=(hbm_space, pl.BlockSpec(memory_space=pltpu.VMEM)),
    )
    cols = exchange(cols, "row")
    rows = lax.all_gather(rows, ("z", "core"))
    away_right, home_right = call(rows_body, (right_shape, right_shape), rows)
    aff_shape = pltpu.VMEM((row * group, lanes), BF16)
    send_shape = shape((half, 48, LANES), F32)
    away_aff, away_send, left, vec = call(
        away_body(log_scale),
        (
            aff_shape,
            send_shape,
            pltpu.VMEM((row * group, LANES), BF16),
            pltpu.VMEM((48, row * group), BF16),
        ),
        away_right,
        cols,
    )
    other = swap(away_send)
    home_aff, home_send = call(home_body(log_scale), (aff_shape, send_shape), left, home_right, vec)
    send = call(join_body, send_shape, home_send, other)
    spread, degree = call(
        scale_body, (shape((row, 40, LANES), F32), shape((16, LANES), F32)), exchange(send, "z")
    )
    away_send, vec, gram = call(
        away_again_body,
        (send_shape, pltpu.VMEM((64, row * group), BF16), pltpu.VMEM((8, LANES), F32)),
        away_aff,
        exchange(spread, "row"),
    )
    other = swap(away_send)
    home_send = call(home_again_body, send_shape, home_aff, vec, gram)
    send = call(join_body, send_shape, home_send, other)
    scaled, gram = call(
        middle_body(total),
        (shape((32, 2 * LANES), F32), shape((col, 8, LANES), F32)),
        exchange(send, "z"),
        degree,
    )
    gram = exchange(gram, ("z", "core"))
    gram = call(again_body, shape((row, 8, LANES), F32), gram)
    out = call(last_body(total), shape((32, group), F32), exchange(gram, "row"), scaled)
    return out.T


def solution(mesh):
    rows, cols = mesh.devices.shape
    finer = Mesh(mesh.devices.reshape(rows, cols // 2, 2), ("row", "z", "core"))
    spec = P(("row", "z", "core"), None)
    return jax.shard_map(
        shards, mesh=finer, in_specs=(spec, spec), out_specs=spec, check_vma=False
    )
```

profile of v0, /device:TPU:1, one launch (start us, length us, event | category | flops | bytes accessed | tf_op | source)
XLA Modules:
  0.0 106.7 jit_solution(18287914146817353419)
XLA Ops:
  0.0 2.0 %shard_map.28 = (bf16[16,200,128]{2,1,0:T(8,128)(2,1)}, bf16[80,128]{1,0:T(8,128)(2,1)S(1)}) custom-call(bf16[64,160]{1,0:T(8,128)(2,1)} %bitcast.5, bf16[32,160]{1,0:T(8,128)(2,1)} %bitcast.6), custom_call_target="tpu_custom_call" | custom-call | tf_op jit(solution)/shard_map/pallas_call | solution.py:374
  2.0 7.6 %all-to-all-start = ((bf16[16,200,128]{2,1,0:T(8,128)(2,1)}), bf16[16,200,128]{2,1,0:T(8,128)(2,1)S(1)}, u32[]{:S(2)}, u32[]{:S(2)}) async-start(bf16[16,200,128]{2,1,0:T(8,128)(2,1)} %get-tuple-element.24), calls=%async_computation | async-start | bytes 1638400 | tf_op jit(solution)/shard_map/all_to_all | solution.py:368
  9.6 21.7 %all-gather = bf16[1280,128]{1,0:T(8,128)(2,1)S(1)} all-gather(bf16[80,128]{1,0:T(8,128)(2,1)S(1)} %get-tuple-element.22), channel_id=2, replica_groups=mesh['row'=16,'z'=8,'core'=2] {'z','core'}, dimensions={0}, use_global_device_ids=true | all-gather | bytes 348160 | tf_op jit(solution)/shard_map/all_gather | solution.py:394
  31.3 0.2 shard_map.29
  31.5 0.0 all-to-all-done.cols_ref
  31.5 2.9 %shard_map.30 = (bf16[2560,1280]{1,0:T(8,128)(2,1)S(1)}, f32[8,48,128]{2,1,0:T(8,128)S(1)}, bf16[2560,128]{1,0:T(8,128)(2,1)S(1)}, bf16[48,2560]{1,0:T(8,128)(2,1)S(1)}) custom-call(bf16[128,1280]{1,0:T(8,128)(2,1)S(1)} %get-tuple-element.23.right_ref, bf16[16,200,128]{2,1,0:T(8,128)(2,1)S(1)} %all-to-all-done.cols_ref), custom_call_target="tpu_custom_call" | custom-call | tf_op jit(solution)/shard_map/pallas_call | solution.py:374
  34.4 0.2 collective-permute-start
  34.6 2.9 %shard_map.31 = (bf16[2560,1280]{1,0:T(8,128)(2,1)S(1)}, f32[8,48,128]{2,1,0:T(8,128)S(1)}) custom-call(bf16[2560,128]{1,0:T(8,128)(2,1)S(1)} %get-tuple-element.25.left_ref, bf16[128,1280]{1,0:T(8,128)(2,1)S(1)} %get-tuple-element.26.right_ref, bf16[48,2560]{1,0:T(8,128)(2,1)S(1)} %get-tuple-element.27.vec_ref), custom_call_target="tpu_custom_call" | custom-call | tf_op jit(solution)/shard_map/pallas_call | solution.py:374
  37.5 0.0 collective-permute-done.other_ref
  37.5 12.6 %all_to_all.30.recv_ref = f32[8,48,128]{2,1,0:T(8,128)S(1)} all-to-all(f32[8,48,128]{2,1,0:T(8,128)S(1)} %shard_map.32), channel_id=1, replica_groups=mesh['row'=16,'z'=8,'core'=2] {'z'}, dimensions={0} | all-to-all | bytes 393216 | tf_op jit(solution)/shard_map/all_to_all | solution.py:368
  50.1 0.1 shard_map.33
  50.2 14.4 %all_to_all.31.spread_ref = f32[16,40,128]{2,1,0:T(8,128)S(1)} all-to-all(f32[16,40,128]{2,1,0:T(8,128)S(1)} %get-tuple-element.32), channel_id=1, replica_groups=mesh['row'=16,'z'=8,'core'=2] {'row'}, dimensions={0} | all-to-all | bytes 655360 | tf_op jit(solution)/shard_map/all_to_all | solution.py:368
  64.6 1.3 %shard_map.34 = (f32[8,48,128]{2,1,0:T(8,128)S(1)}, bf16[64,2560]{1,0:T(8,128)(2,1)S(1)}, f32[8,128]{1,0:T(8,128)S(1)}) custom-call(bf16[2560,1280]{1,0:T(8,128)(2,1)S(1)} %get-tuple-element.29.aff_ref, f32[16,40,128]{2,1,0:T(8,128)S(1)} %all_to_all.31.spread_ref), custom_call_target="tpu_custom_call" | custom-call | tf_op jit(solution)/shard_map/pallas_call | solution.py:374
  65.9 3.5 %collective-permute-start.1 = (f32[8,48,128]{2,1,0:T(8,128)S(1)}, f32[8,48,128]{2,1,0:T(8,128)S(1)}, u32[]{:S(2)}, u32[]{:S(2)}) collective-permute-start(f32[8,48,128]{2,1,0:T(8,128)S(1)} %get-tuple-element.35), channel_id=1, source_target_pairs={{0,1},{1,0},{2,3},{3,2},{4,5},{5,4},{6,7},{7,6},{8,9},{9,8},{10,11... | collective-permute-start | bytes 589832 | tf_op jit(solution)/shard_map/ppermute | solution.py:371
  69.4 1.2 %shard_map.35.mine_ref = f32[8,48,128]{2,1,0:T(8,128)S(1)} custom-call(bf16[2560,1280]{1,0:T(8,128)(2,1)S(1)} %get-tuple-element.28.aff_ref, bf16[64,2560]{1,0:T(8,128)(2,1)S(1)} %get-tuple-element.33.vec_ref, f32[8,128]{1,0:T(8,128)S(1)} %get-tuple-element.34.gram_ref), custom_call_target="tpu_custom_call" | custom-call | tf_op jit(solution)/shard_map/pallas_call | solution.py:374
  70.6 0.0 collective-permute-done.1.other_ref
  70.7 13.3 %all_to_all.32.recv_ref = f32[8,48,128]{2,1,0:T(8,128)S(1)} all-to-all(f32[8,48,128]{2,1,0:T(8,128)S(1)} %shard_map.36), channel_id=1, replica_groups=mesh['row'=16,'z'=8,'core'=2] {'z'}, dimensions={0} | all-to-all | bytes 393216 | tf_op jit(solution)/shard_map/all_to_all | solution.py:368
  84.0 0.9 shard_map.37
  84.9 10.7 %all_to_all.33.recv_ref = f32[16,8,128]{2,1,0:T(8,128)S(1)} all-to-all(f32[16,8,128]{2,1,0:T(8,128)S(1)} %get-tuple-element.37), channel_id=1, replica_groups=mesh['row'=16,'z'=8,'core'=2] {'z','core'}, dimensions={0} | all-to-all | bytes 131072 | tf_op jit(solution)/shard_map/all_to_all | solution.py:368
  95.7 9.7 %all_to_all.34.recv_ref = f32[16,8,128]{2,1,0:T(8,128)S(1)} all-to-all(f32[16,8,128]{2,1,0:T(8,128)S(1)} %shard_map.38), channel_id=1, replica_groups=mesh['row'=16,'z'=8,'core'=2] {'row'}, dimensions={0} | all-to-all | bytes 131072 | tf_op jit(solution)/shard_map/all_to_all | solution.py:368
  105.4 1.3 %shard_map.39 = f32[32,160]{1,0:T(8,128)} custom-call(f32[16,8,128]{2,1,0:T(8,128)S(1)} %all_to_all.34.recv_ref, f32[32,256]{1,0:T(8,128)S(1)} %get-tuple-element.38.scaled_ref), custom_call_target="tpu_custom_call" | custom-call | tf_op jit(solution)/shard_map/pallas_call | solution.py:374
  (3 shorter events, 0.1 us)
Async XLA Ops:
  2.0 29.5 %all-to-all-start = ((bf16[16,200,128]{2,1,0:T(8,128)(2,1)}), bf16[16,200,128]{2,1,0:T(8,128)(2,1)S(1)}, u32[]{:S(2)}, u32[]{:S(2)}) async-start(bf16[16,200,128]{2,1,0:T(8,128)(2,1)} %get-tuple-element.24), calls=%async_computation | async-start | bytes 1638400 | tf_op jit(solution)/shard_map/all_to_all | solution.py:368
  34.4 3.1 %collective-permute-start = (f32[8,48,128]{2,1,0:T(8,128)S(1)}, f32[8,48,128]{2,1,0:T(8,128)S(1)}, u32[]{:S(2)}, u32[]{:S(2)}) collective-permute-start(f32[8,48,128]{2,1,0:T(8,128)S(1)} %get-tuple-element.31), channel_id=1, source_target_pairs={{0,1},{1,0},{2,3},{3,2},{4,5},{5,4},{6,7},{7,6},{8,9},{9,8},{10,11... | collective-permute-start | bytes 589832 | tf_op jit(solution)/shard_map/ppermute | solution.py:371
  65.9 4.7 %collective-permute-start.1 = (f32[8,48,128]{2,1,0:T(8,128)S(1)}, f32[8,48,128]{2,1,0:T(8,128)S(1)}, u32[]{:S(2)}, u32[]{:S(2)}) collective-permute-start(f32[8,48,128]{2,1,0:T(8,128)S(1)} %get-tuple-element.35), channel_id=1, source_target_pairs={{0,1},{1,0},{2,3},{3,2},{4,5},{5,4},{6,7},{7,6},{8,9},{9,8},{10,11... | collective-permute-start | bytes 589832 | tf_op jit(solution)/shard_map/ppermute | solution.py:371
where the time goes:
time: 107 us
  blocking collectives  82.4 us (77%)
  Pallas kernels  12.9 us (12%)
  starting transfers between devices  11.3 us (11%)
    all_to_all x5, blocking collectives, exchange(): return lax.all_to_all(x, axis, 0, 0, tiled=True)  60.7 us
    all_gather x1, blocking collectives, shards(): rows = lax.all_gather(rows, ('z', 'core'))  21.7 us
    pallas_call x12, Pallas kernels, call(): pl.pallas_call(body, out_shape=out_shape, scratch_shapes=scratch, compile...  12.9 us
    all_to_all x1, starting transfers between devices, exchange(): return lax.all_to_all(x, axis, 0, 0, tiled=True)  7.58 us
    ppermute x2, starting transfers between devices, swap(): return lax.ppermute(x, 'core', [(0, 1), (1, 0)])  3.71 us
  transfers between devices with their start and end apart: 3, of which 0 were waited for; matrix products, arithmetic and copies ran while one was open for 0% of the time, Pallas kernels for 4%

commit v1 on v0

--- a/solution.py
+++ b/solution.py
@@ -78,7 +78,8 @@
     )
     for load in loads:
         load.start()
-    loads[0].wait()
+    for load in loads:
+        load.wait()
     pts = points_ref[...].astype(F32)
     group = pts.shape[1]
     main, rest = main_and_rest(pts)
@@ -91,9 +92,9 @@
         extra = jnp.where(row == k, piece, extra)
     blank = jnp.zeros((LANES - NORM - 8, flat.shape[1]), F32)
     flat = jnp.concatenate([flat, extra, blank], axis=0).T[0:group]
-    loads[1].wait()
     main, rest = main_and_rest(vectors_ref[...].astype(F32))
-    block_ref[...] = jnp.concatenate([flat, main, rest], axis=0).astype(BF16)
+    block_ref[group:, :] = jnp.concatenate([main, rest], axis=0).astype(BF16)
+    block_ref[0:group, :] = flat.astype(BF16)
     count = cols_hbm.shape[0]
     sends = [
         pltpu.make_async_copy(block_ref, cols_hbm.at[i], sems.at[2 + i]) for i in range(count)
@@ -191,7 +192,8 @@
 
 
 def away_body(log_scale):
-    def body(right_ref, cols_ref, aff_ref, send_ref, left_ref, vec_ref):
+    def body(rows_ref, cols_ref, aff_ref, send_ref, left_ref, vec_ref, right_ref):
+        put_rows(rows_ref, 1 - lax.axis_index("core"), right_ref)
         put_columns(cols_ref, left_ref, vec_ref)
         affinity_product(log_scale, left_ref, right_ref, vec_ref, aff_ref, send_ref)
 
@@ -199,16 +201,11 @@
 
 
 def home_body(log_scale):
-    def body(left_ref, right_ref, vec_ref, aff_ref, send_ref):
+    def body(rows_ref, left_ref, vec_ref, aff_ref, send_ref, right_ref):
+        put_rows(rows_ref, lax.axis_index("core"), right_ref)
         affinity_product(log_scale, left_ref, right_ref, vec_ref, aff_ref, send_ref)
 
     return body
-
-
-def rows_body(rows_ref, away_right_ref, home_right_ref):
-    core = lax.axis_index("core")
-    put_rows(rows_ref, 1 - core, away_right_ref)
-    put_rows(rows_ref, core, home_right_ref)
 
 
 def join_body(mine_ref, other_ref, out_ref):
@@ -392,7 +389,6 @@
     )
     cols = exchange(cols, "row")
     rows = lax.all_gather(rows, ("z", "core"))
-    away_right, home_right = call(rows_body, (right_shape, right_shape), rows)
     aff_shape = pltpu.VMEM((row * group, lanes), BF16)
     send_shape = shape((half, 48, LANES), F32)
     away_aff, away_send, left, vec = call(
@@ -403,11 +399,14 @@
             pltpu.VMEM((row * group, LANES), BF16),
             pltpu.VMEM((48, row * group), BF16),
         ),
-        away_right,
+        rows,
         cols,
+        scratch=(right_shape,),
     )
     other = swap(away_send)
-    home_aff, home_send = call(home_body(log_scale), (aff_shape, send_shape), left, home_right, vec)
+    home_aff, home_send = call(
+        home_body(log_scale), (aff_shape, send_shape), rows, left, vec, scratch=(right_shape,)
+    )
     send = call(join_body, send_shape, home_send, other)
     spread, degree = call(
         scale_body, (shape((row, 40, LANES), F32), shape((16, LANES), F32)), exchange(send, "z")

time: 107 us -> 107 us (level)
    pallas_call x12 -> x11, Pallas kernels: 12.9 us -> 12.8 us  [call(): pl.pallas_call(body, out_shape=out_shape, scratch_shapes=scratch, compile...]
where the time goes in v1:
time: 107 us
  blocking collectives  82.4 us (77%)
  Pallas kernels  12.8 us (12%)
  starting transfers between devices  11.3 us (11%)
    all_to_all x5, blocking collectives, exchange(): return lax.all_to_all(x, axis, 0, 0, tiled=True)  60.8 us
    all_gather x1, blocking collectives, shards(): rows = lax.all_gather(rows, ('z', 'core'))  21.7 us
    pallas_call x11, Pallas kernels, call(): pl.pallas_call(body, out_shape=out_shape, scratch_shapes=scratch, compile...  12.8 us
    all_to_all x1, starting transfers between devices, exchange(): return lax.all_to_all(x, axis, 0, 0, tiled=True)  7.58 us
    ppermute x2, starting transfers between devices, swap(): return lax.ppermute(x, 'core', [(0, 1), (1, 0)])  3.71 us
  transfers between devices with their start and end apart: 3, of which 0 were waited for; matrix products, arithmetic and copies ran while one was open for 0% of the time, Pallas kernels for 4%

profile of v1, /device:TPU:1, one launch (start us, length us, event | category | flops | bytes accessed | tf_op | source)
XLA Modules:
  0.0 106.6 jit_solution(10871126695733595079)
XLA Ops:
  0.0 1.9 %shard_map.28 = (bf16[16,200,128]{2,1,0:T(8,128)(2,1)}, bf16[80,128]{1,0:T(8,128)(2,1)S(1)}) custom-call(bf16[64,160]{1,0:T(8,128)(2,1)} %bitcast.6, bf16[32,160]{1,0:T(8,128)(2,1)} %bitcast.7), custom_call_target="tpu_custom_call" | custom-call | tf_op jit(solution)/shard_map/pallas_call | solution.py:371
  1.9 7.6 %all-to-all-start = ((bf16[16,200,128]{2,1,0:T(8,128)(2,1)}), bf16[16,200,128]{2,1,0:T(8,128)(2,1)S(1)}, u32[]{:S(2)}, u32[]{:S(2)}) async-start(bf16[16,200,128]{2,1,0:T(8,128)(2,1)} %get-tuple-element.21), calls=%async_computation | async-start | bytes 1638400 | tf_op jit(solution)/shard_map/all_to_all | solution.py:365
  9.5 21.7 %all-gather = bf16[1280,128]{1,0:T(8,128)(2,1)S(1)} all-gather(bf16[80,128]{1,0:T(8,128)(2,1)S(1)} %get-tuple-element.20), channel_id=2, replica_groups=mesh['row'=16,'z'=8,'core'=2] {'z','core'}, dimensions={0}, use_global_device_ids=true | all-gather | bytes 348160 | tf_op jit(solution)/shard_map/all_gather | solution.py:391
  31.2 0.0 all-to-all-done.cols_ref
  31.2 3.0 %shard_map.29 = (bf16[2560,1280]{1,0:T(8,128)(2,1)S(1)}, f32[8,48,128]{2,1,0:T(8,128)S(1)}, bf16[2560,128]{1,0:T(8,128)(2,1)S(1)}, bf16[48,2560]{1,0:T(8,128)(2,1)S(1)}) custom-call(bf16[16,80,128]{2,1,0:T(8,128)(2,1)S(1)} %bitcast.4, bf16[16,200,128]{2,1,0:T(8,128)(2,1)S(1)} %all-to-all-done.cols_ref), custom_call_target="tpu_custom_call" | custom-call | tf_op jit(solution)/shard_map/pallas_call | solution.py:371
  34.2 0.2 collective-permute-start
  34.4 2.9 %shard_map.30 = (bf16[2560,1280]{1,0:T(8,128)(2,1)S(1)}, f32[8,48,128]{2,1,0:T(8,128)S(1)}) custom-call(bf16[16,80,128]{2,1,0:T(8,128)(2,1)S(1)} %bitcast.5, bf16[2560,128]{1,0:T(8,128)(2,1)S(1)} %get-tuple-element.22.left_ref, bf16[48,2560]{1,0:T(8,128)(2,1)S(1)} %get-tuple-element.23.vec_ref), custom_call_target="tpu_custom_call" | custom-call | tf_op jit(solution)/shard_map/pallas_call | solution.py:371
  37.4 0.0 collective-permute-done.other_ref
  37.4 12.6 %all_to_all.30.recv_ref = f32[8,48,128]{2,1,0:T(8,128)S(1)} all-to-all(f32[8,48,128]{2,1,0:T(8,128)S(1)} %shard_map.31), channel_id=1, replica_groups=mesh['row'=16,'z'=8,'core'=2] {'z'}, dimensions={0} | all-to-all | bytes 393216 | tf_op jit(solution)/shard_map/all_to_all | solution.py:365
  50.0 0.1 shard_map.32
  50.1 14.4 %all_to_all.31.spread_ref = f32[16,40,128]{2,1,0:T(8,128)S(1)} all-to-all(f32[16,40,128]{2,1,0:T(8,128)S(1)} %get-tuple-element.28), channel_id=1, replica_groups=mesh['row'=16,'z'=8,'core'=2] {'row'}, dimensions={0} | all-to-all | bytes 655360 | tf_op jit(solution)/shard_map/all_to_all | solution.py:365
  64.5 1.3 %shard_map.33 = (f32[8,48,128]{2,1,0:T(8,128)S(1)}, bf16[64,2560]{1,0:T(8,128)(2,1)S(1)}, f32[8,128]{1,0:T(8,128)S(1)}) custom-call(bf16[2560,1280]{1,0:T(8,128)(2,1)S(1)} %get-tuple-element.25.aff_ref, f32[16,40,128]{2,1,0:T(8,128)S(1)} %all_to_all.31.spread_ref), custom_call_target="tpu_custom_call" | custom-call | tf_op jit(solution)/shard_map/pallas_call | solution.py:371
  65.8 3.5 %collective-permute-start.1 = (f32[8,48,128]{2,1,0:T(8,128)S(1)}, f32[8,48,128]{2,1,0:T(8,128)S(1)}, u32[]{:S(2)}, u32[]{:S(2)}) collective-permute-start(f32[8,48,128]{2,1,0:T(8,128)S(1)} %get-tuple-element.31), channel_id=1, source_target_pairs={{0,1},{1,0},{2,3},{3,2},{4,5},{5,4},{6,7},{7,6},{8,9},{9,8},{10,11... | collective-permute-start | bytes 589832 | tf_op jit(solution)/shard_map/ppermute | solution.py:368
  69.3 1.2 %shard_map.34.mine_ref = f32[8,48,128]{2,1,0:T(8,128)S(1)} custom-call(bf16[2560,1280]{1,0:T(8,128)(2,1)S(1)} %get-tuple-element.24.aff_ref, bf16[64,2560]{1,0:T(8,128)(2,1)S(1)} %get-tuple-element.29.vec_ref, f32[8,128]{1,0:T(8,128)S(1)} %get-tuple-element.30.gram_ref), custom_call_target="tpu_custom_call" | custom-call | tf_op jit(solution)/shard_map/pallas_call | solution.py:371
  70.5 0.0 collective-permute-done.1.other_ref
  70.6 13.3 %all_to_all.32.recv_ref = f32[8,48,128]{2,1,0:T(8,128)S(1)} all-to-all(f32[8,48,128]{2,1,0:T(8,128)S(1)} %shard_map.35), channel_id=1, replica_groups=mesh['row'=16,'z'=8,'core'=2] {'z'}, dimensions={0} | all-to-all | bytes 393216 | tf_op jit(solution)/shard_map/all_to_all | solution.py:365
  83.9 0.9 shard_map.36
  84.8 10.7 %all_to_all.33.recv_ref = f32[16,8,128]{2,1,0:T(8,128)S(1)} all-to-all(f32[16,8,128]{2,1,0:T(8,128)S(1)} %get-tuple-element.33), channel_id=1, replica_groups=mesh['row'=16,'z'=8,'core'=2] {'z','core'}, dimensions={0} | all-to-all | bytes 131072 | tf_op jit(solution)/shard_map/all_to_all | solution.py:365
  95.6 9.7 %all_to_all.34.recv_ref = f32[16,8,128]{2,1,0:T(8,128)S(1)} all-to-all(f32[16,8,128]{2,1,0:T(8,128)S(1)} %shard_map.37), channel_id=1, replica_groups=mesh['row'=16,'z'=8,'core'=2] {'row'}, dimensions={0} | all-to-all | bytes 131072 | tf_op jit(solution)/shard_map/all_to_all | solution.py:365
  105.2 1.3 %shard_map.38 = f32[32,160]{1,0:T(8,128)} custom-call(f32[16,8,128]{2,1,0:T(8,128)S(1)} %all_to_all.34.recv_ref, f32[32,256]{1,0:T(8,128)S(1)} %get-tuple-element.34.scaled_ref), custom_call_target="tpu_custom_call" | custom-call | tf_op jit(solution)/shard_map/pallas_call | solution.py:371
  (3 shorter events, 0.1 us)
Async XLA Ops:
  1.9 29.3 %all-to-all-start = ((bf16[16,200,128]{2,1,0:T(8,128)(2,1)}), bf16[16,200,128]{2,1,0:T(8,128)(2,1)S(1)}, u32[]{:S(2)}, u32[]{:S(2)}) async-start(bf16[16,200,128]{2,1,0:T(8,128)(2,1)} %get-tuple-element.21), calls=%async_computation | async-start | bytes 1638400 | tf_op jit(solution)/shard_map/all_to_all | solution.py:365
  34.2 3.2 %collective-permute-start = (f32[8,48,128]{2,1,0:T(8,128)S(1)}, f32[8,48,128]{2,1,0:T(8,128)S(1)}, u32[]{:S(2)}, u32[]{:S(2)}) collective-permute-start(f32[8,48,128]{2,1,0:T(8,128)S(1)} %get-tuple-element.27), channel_id=1, source_target_pairs={{0,1},{1,0},{2,3},{3,2},{4,5},{5,4},{6,7},{7,6},{8,9},{9,8},{10,11... | collective-permute-start | bytes 589832 | tf_op jit(solution)/shard_map/ppermute | solution.py:368
  65.8 4.7 %collective-permute-start.1 = (f32[8,48,128]{2,1,0:T(8,128)S(1)}, f32[8,48,128]{2,1,0:T(8,128)S(1)}, u32[]{:S(2)}, u32[]{:S(2)}) collective-permute-start(f32[8,48,128]{2,1,0:T(8,128)S(1)} %get-tuple-element.31), channel_id=1, source_target_pairs={{0,1},{1,0},{2,3},{3,2},{4,5},{5,4},{6,7},{7,6},{8,9},{9,8},{10,11... | collective-permute-start | bytes 589832 | tf_op jit(solution)/shard_map/ppermute | solution.py:368
